TPU v7x, 256 devices: a whole 4x4x8 slice. The times are simulated.
256 devices in a mesh: grp: 16 (over y, z_lo, core), sp: 16 (over z_hi, x).
Axes of the slice: x: 4, y: 4, z: 8 (z_hi: 4, z_lo: 2; z = z_hi * 2 + z_lo), core: 2. Of those that a mesh axis runs over, the one named last changes fastest.
Arguments:
- bucket_of: int32 [16], replicated, may hold values from 0 to 3, as said below
- lengths: int32 [4], replicated, may hold values from 256 to 1024, as said below
- counts: int32 [4], replicated, may hold values from 256 to 4096
- queries: bfloat16 [32768, 4096], P(('grp', 'sp')), may hold values from -4.5 to 4.5
- keys: bfloat16 [32768, 4096], P(('grp', 'sp')), may hold values from -4.5 to 4.5
- values: bfloat16 [32768, 4096], P(('grp', 'sp')), may hold values from -6 to 6
- out_grad: bfloat16 [32768, 3072], P(('grp', 'sp')), may hold values from -24 to 24
- w_out: bfloat16 [4096, 3072], P('sp', 'grp'), may hold values from -1.75 to 1.75
Outputs:
- grad_queries: bfloat16 [32768, 4096], P(('grp', 'sp'))
- grad_keys: bfloat16 [32768, 4096], P(('grp', 'sp'))
- grad_values: bfloat16 [32768, 4096], P(('grp', 'sp'))
- grad_w_out: float32 [4096, 3072], P('sp', 'grp')
Inputs may be any that keep to these rules, and one draw needn't show every extreme that they name: `bucket_of`: every one of the 4 buckets is held by at least one group. `lengths`: one bucket has length exactly 1024.
All inputs are finite; a program needn't handle non-finite values.
Results may differ from a plain program's by a relative error of at most 0.0091.
Values may be sent and summed in bfloat16 or wider, within the bound.
A program may use at most 128 MiB of HBM per device.

v0:
```python
import jax
import jax.numpy as jnp
from jax import lax
from jax.sharding import PartitionSpec as P

HEAD_DIM = 128
SEQS = 2


def copy_for_each(shard, axis):
    devices = lax.axis_size(axis)
    return lax.all_to_all(
        jnp.broadcast_to(shard[None], (devices, *shard.shape)), axis, 0, 0, tiled=True
    )


def joined_along(pieces, dim):
    lengths = list(pieces.shape[1:])
    lengths[dim] *= pieces.shape[0]
    return jnp.moveaxis(pieces, 0, dim).reshape(lengths)


def gather_directly(shard, axis, dim):
    pieces = copy_for_each(shard, axis)
    return joined_along(pieces, dim)


def dot_nt(first_op, second_op):
    return lax.dot_general(
        first_op, second_op, (((1,), (1,)), ((), ())), preferred_element_type=jnp.float32
    )


def dot_tn(first_op, second_op):
    return lax.dot_general(
        first_op, second_op, (((0,), (0,)), ((), ())), preferred_element_type=jnp.float32
    )


def probabilities(query_rows, key_rows, keep_cols):
    scores = dot_nt(query_rows, key_rows) * query_rows.shape[1] ** (-0.5)
    scores = jnp.where(keep_cols[None, :], scores, -jnp.inf)
    row_top = jnp.max(scores, axis=1, keepdims=True)
    row_exp = jnp.exp(scores - row_top)
    return row_exp / jnp.sum(row_exp, axis=1, keepdims=True)


def shards(bucket_of, lengths, counts, queries, keys, values, out_grad, w_out):
    group_index = lax.axis_index("grp")
    number_groups = lax.axis_size("grp")
    bucket_count = lengths.shape[0]
    bucket_table = (
        bucket_of[:, None] == jnp.arange(bucket_count, dtype=jnp.int32)[None, :]
    ).astype(jnp.int32)
    group_counts = jnp.sum(bucket_table * counts[None, :], axis=1)
    group_lengths = jnp.sum(bucket_table * lengths[None, :], axis=1)
    own_group = (jnp.arange(number_groups, dtype=jnp.int32) == group_index).astype(jnp.int32)
    seq_len = jnp.sum(own_group * group_lengths)
    weight = jnp.sum(own_group * group_counts).astype(jnp.float32) / jnp.sum(group_counts).astype(
        jnp.float32
    )
    heads_q, heads_k, heads_v = (
        lax.all_to_all(queries, "sp", split_axis=1, concat_axis=0, tiled=True),
        lax.all_to_all(keys, "sp", split_axis=1, concat_axis=0, tiled=True),
        lax.all_to_all(values, "sp", split_axis=1, concat_axis=0, tiled=True),
    )
    group_rows = heads_q.shape[0]
    width_local = heads_q.shape[1]
    capacity = group_rows // SEQS
    local_heads = width_local // HEAD_DIM
    item_count = SEQS * local_heads
    keep_cols = jnp.arange(capacity, dtype=jnp.int32) < seq_len
    keep_rows = jnp.tile(keep_cols, SEQS)
    row_scale = keep_rows[:, None].astype(jnp.float32)

    def item_corner(item_index):
        return (item_index // local_heads * capacity, item_index % local_heads * HEAD_DIM)

    def take_item(source, row_first, col_first):
        return lax.dynamic_slice(source, (row_first, col_first), (capacity, HEAD_DIM))

    def forward_item(item_index, attn_all):
        row_first, col_first = item_corner(item_index)
        query_rows = take_item(heads_q, row_first, col_first)
        key_rows = take_item(heads_k, row_first, col_first)
        value_rows = take_item(heads_v, row_first, col_first)
        probs_low = probabilities(query_rows, key_rows, keep_cols).astype(jnp.bfloat16)
        attn_item = jnp.dot(probs_low, value_rows, preferred_element_type=jnp.float32).astype(
            jnp.bfloat16
        )
        return lax.dynamic_update_slice(attn_all, attn_item, (row_first, col_first))

    attention = lax.fori_loop(
        0, item_count, forward_item, jnp.zeros((group_rows, width_local), jnp.bfloat16)
    )
    masked = attention * keep_rows[:, None].astype(jnp.bfloat16)
    w_rows = gather_directly(w_out, "grp", 1)
    gathered = lax.all_gather(out_grad, "sp", axis=0, tiled=True)
    d_full = dot_nt(gathered, w_rows)
    grad_local = dot_tn(masked, gathered)
    d_attn = (d_full * row_scale).astype(jnp.bfloat16)

    def backward_item(item_index, grad_heads):
        grad_q_all, grad_k_all, grad_v_all = grad_heads
        row_first, col_first = item_corner(item_index)
        query_rows = take_item(heads_q, row_first, col_first)
        key_rows = take_item(heads_k, row_first, col_first)
        value_rows = take_item(heads_v, row_first, col_first)
        attn_item = take_item(attention, row_first, col_first)
        d_item = take_item(d_attn, row_first, col_first)
        probs_full = probabilities(query_rows, key_rows, keep_cols)
        probs_low = probs_full.astype(jnp.bfloat16)
        row_delta = jnp.sum(
            d_item.astype(jnp.float32) * attn_item.astype(jnp.float32), axis=1, keepdims=True
        )
        dscore = (probs_full * (dot_nt(d_item, value_rows) - row_delta)).astype(jnp.bfloat16)
        factor = HEAD_DIM ** (-0.5)
        grad_q = (jnp.dot(dscore, key_rows, preferred_element_type=jnp.float32) * factor).astype(
            jnp.bfloat16
        )
        grad_k = (dot_tn(dscore, query_rows) * factor).astype(jnp.bfloat16)
        grad_v = dot_tn(probs_low, d_item).astype(jnp.bfloat16)
        grad_q_all = lax.dynamic_update_slice(grad_q_all, grad_q, (row_first, col_first))
        grad_k_all = lax.dynamic_update_slice(grad_k_all, grad_k, (row_first, col_first))
        grad_v_all = lax.dynamic_update_slice(grad_v_all, grad_v, (row_first, col_first))
        return (grad_q_all, grad_k_all, grad_v_all)

    empty_heads = jnp.zeros((group_rows, width_local), jnp.bfloat16)
    grad_q_all, grad_k_all, grad_v_all = lax.fori_loop(
        0, item_count, backward_item, (empty_heads, empty_heads, empty_heads)
    )
    back_q, back_k, back_v = (
        lax.all_to_all(grad_q_all, "sp", split_axis=0, concat_axis=1, tiled=True),
        lax.all_to_all(grad_k_all, "sp", split_axis=0, concat_axis=1, tiled=True),
        lax.all_to_all(grad_v_all, "sp", split_axis=0, concat_axis=1, tiled=True),
    )
    weighted = weight * grad_local
    grad_w = lax.psum_scatter(weighted, "grp", scatter_dimension=1, tiled=True)
    return (back_q, back_k, back_v, grad_w)


def solution(mesh):
    in_specs = (
        P(),
        P(),
        P(),
        P(("grp", "sp"), None),
        P(("grp", "sp"), None),
        P(("grp", "sp"), None),
        P(("grp", "sp"), None),
        P("sp", "grp"),
    )
    out_specs = (
        P(("grp", "sp"), None),
        P(("grp", "sp"), None),
        P(("grp", "sp"), None),
        P("sp", "grp"),
    )
    return jax.shard_map(shards, mesh=mesh, in_specs=in_specs, out_specs=out_specs, check_vma=False)
```

profile of v0, /device:TPU:8, one launch (start us, length us, event | category | flops | bytes accessed | tf_op | source)
XLA Modules:
  0.0 414.1 jit_solution(11999893446016128008)
XLA Ops:
  7.9 2.4 copy.64
  10.3 11.0 %all-to-all-start = ((bf16[128,16,256]{2,0,1:T(8,128)(2,1)}), bf16[128,16,256]{2,0,1:T(8,128)(2,1)S(1)}, u32[]{:S(2)}, u32[]{:S(2)}) async-start(bf16[128,16,256]{2,0,1:T(8,128)(2,1)} %bitcast.48), calls=%async_computation | async-start | bytes 2097152 | tf_op jit(solution)/shard_map/all_to_all | solution.py:63
  21.4 1.1 copy.63
  22.5 35.2 %all-to-all-done = bf16[128,16,256]{2,0,1:T(8,128)(2,1)S(1)} async-done(((bf16[128,16,256]{2,0,1:T(8,128)(2,1)}), bf16[128,16,256]{2,0,1:T(8,128)(2,1)S(1)}, u32[]{:S(2)}, u32[]{:S(2)}) %all-to-all-start) | async-done | bytes 1048608 | tf_op jit(solution)/shard_map/all_to_all | solution.py:63
  57.7 12.6 %all-to-all-start.1 = ((bf16[128,16,256]{2,0,1:T(8,128)(2,1)}), bf16[128,16,256]{2,0,1:T(8,128)(2,1)S(1)}, u32[]{:S(2)}, u32[]{:S(2)}) async-start(bf16[128,16,256]{2,0,1:T(8,128)(2,1)} %bitcast.47), calls=%async_computation.1 | async-start | bytes 2097152 | tf_op jit(solution)/shard_map/all_to_all | solution.py:64
  70.3 1.1 copy.62
  71.4 27.0 %all-to-all-done.1 = bf16[128,16,256]{2,0,1:T(8,128)(2,1)S(1)} async-done(((bf16[128,16,256]{2,0,1:T(8,128)(2,1)}), bf16[128,16,256]{2,0,1:T(8,128)(2,1)S(1)}, u32[]{:S(2)}, u32[]{:S(2)}) %all-to-all-start.1) | async-done | bytes 1048608 | tf_op jit(solution)/shard_map/all_to_all | solution.py:64
  98.4 6.2 %all-to-all-start.3 = ((bf16[128,16,256]{2,0,1:T(8,128)(2,1)}), bf16[128,16,256]{2,0,1:T(8,128)(2,1)S(1)}, u32[]{:S(2)}, u32[]{:S(2)}) async-start(bf16[128,16,256]{2,0,1:T(8,128)(2,1)} %bitcast.46), calls=%async_computation.3 | async-start | bytes 2097152 | tf_op jit(solution)/shard_map/all_to_all | solution.py:65
  108.6 45.1 %all-to-all-done.3 = bf16[128,16,256]{2,0,1:T(8,128)(2,1)S(1)} async-done(((bf16[128,16,256]{2,0,1:T(8,128)(2,1)}), bf16[128,16,256]{2,0,1:T(8,128)(2,1)S(1)}, u32[]{:S(2)}, u32[]{:S(2)}) %all-to-all-start.3) | async-done | bytes 1048608 | tf_op jit(solution)/shard_map/all_to_all | solution.py:65
  153.8 1.5 broadcast_in_dim.87
  155.2 7.9 %all-to-all-start.2 = ((bf16[16,256,192]{1,2,0:T(8,128)(2,1)}), bf16[16,256,192]{1,2,0:T(8,128)(2,1)}, u32[]{:S(2)}, u32[]{:S(2)}) async-start(bf16[16,256,192]{1,2,0:T(8,128)(2,1)} %broadcast_in_dim.87), calls=%async_computation.2 | async-start | bytes 3145728 | tf_op jit(solution)/shard_map/all_to_all | solution.py:12
  163.2 19.5 %while.36 = (s32[]{:T(128)}, bf16[2048,256]{1,0:T(8,128)(2,1)S(1)}, bf16[2048,256]{1,0:T(8,128)(2,1)S(1)}, bf16[2048,256]{1,0:T(8,128)(2,1)S(1)}, bf16[2048,256]...) while((s32[]{:T(128)}, bf16[2048,256]{1,0:T(8,128)(2,1)S(1)}, ...), condition=%wide.region_5.6_spmd.clone, body=%wide.region_2.5_spmd.clone.sunk | while | flops 549583872 | bytes 13660512 | solution.py:93
  163.9 0.7 fusion.69
  164.6 0.9 fusion.70
  165.5 2.5 fusion.71
  168.8 0.7 fusion.69
  169.5 0.9 fusion.70
  170.4 2.5 fusion.71
  173.6 0.7 fusion.69
  174.4 0.9 fusion.70
  175.3 2.5 fusion.71
  178.5 0.7 fusion.69
  179.2 0.9 fusion.70
  180.1 2.5 fusion.71
  182.7 56.8 %all-gather.2.cloned.1.call-done = bf16[2048,3072]{1,0:T(8,128)(2,1)} async-done(((bf16[128,3072]{1,0:T(8,128)(2,1)}), bf16[2048,3072]{1,0:T(8,128)(2,1)}) %all-gather.2.cloned.1.call-update) | async-done | bytes 12582928 | tf_op jit(solution)/shard_map/all_gather | solution.py:98
  239.5 11.6 %convolution_multiply_fusion.2 = f32[256,3072]{0,1:T(8,128)} fusion(bf16[2048,3072]{1,0:T(8,128)(2,1)} %all-gather.2.cloned.1.call-done, f32[]{:T(128)S(6)} %div.66, bf16[2048,256]{1,0:T(8,128)(2,1)S(1)} %get-tuple-element.655, bf16[2048]{0:T(1024)(128)(2,1)S(1)} %bitcast.67), kind=kOutput, calls=%fused_computation.43 | convolution fusion | flops 3222536192 | bytes 16781316 | tf_op jit(solution)/shard_map/dot_general | solution.py:35
  251.1 9.5 %fusion.39 = bf16[2048,256]{1,0:T(8,128)(2,1)} fusion(bf16[2048,3072]{1,0:T(8,128)(2,1)} %all-gather.2.cloned.1.call-done, bf16[256,3072]{0,1:T(8,128)(2,1)} %bitcast.5, f32[2048]{0:T(1024)S(1)} %bitcast.66), kind=kOutput, calls=%fused_computation.45 | convolution fusion | flops 3222274048 | bytes 15212544 | tf_op jit(solution)/shard_map/dot_general | solution.py:29
  260.5 1.0 broadcast.62.clone.1
  261.6 1.0 broadcast.62.clone
  262.6 1.0 broadcast.62
  263.7 42.5 %while.37 = (s32[]{:T(128)}, bf16[2048,256]{1,0:T(8,128)(2,1)}, bf16[2048,256]{1,0:T(8,128)(2,1)}, bf16[2048,256]{1,0:T(8,128)(2,1)}, bf16[2048,256]{1,0:T(8,128...) while((s32[]{:T(128)}, bf16[2048,256]{1,0:T(8,128)(2,1)}, ...), condition=%wide.region_10.11_spmd.clone, body=%wide.region_6.10_spmd.clone.sunk | while | flops 1363277824 | bytes 30461348 | solution.py:129
  264.3 1.2 multiply_reduce_fusion.2
  266.2 0.9 fusion.81
  267.1 1.9 fusion.84
  269.0 2.4 multiply_convert_fusion.2
  271.4 1.4 fusion.83
  272.8 1.5 fusion.82
  274.9 1.2 multiply_reduce_fusion.2
  276.1 0.7 fusion.80
  276.8 0.9 fusion.81
  277.8 1.9 fusion.84
  279.7 2.4 multiply_convert_fusion.2
  282.0 1.4 fusion.83
  283.4 1.5 fusion.82
  285.6 1.2 multiply_reduce_fusion.2
  287.5 0.9 fusion.81
  288.4 1.9 fusion.84
  290.3 2.4 multiply_convert_fusion.2
  292.6 1.4 fusion.83
  294.1 1.5 fusion.82
  296.2 1.2 multiply_reduce_fusion.2
  298.1 0.9 fusion.81
  299.0 1.9 fusion.84
  300.9 2.4 multiply_convert_fusion.2
  303.3 1.4 fusion.83
  304.7 1.5 fusion.82
  306.2 33.9 %all_to_all.119 = bf16[16,128,256]{2,1,0:T(8,128)(2,1)S(1)} all-to-all(bf16[16,128,256]{2,1,0:T(8,128)(2,1)} %bitcast.58), channel_id=1, replica_groups=mesh['grp'=16,'sp'=16] {'sp'}, dimensions={0} | all-to-all | bytes 2097152 | tf_op jit(solution)/shard_map/all_to_all | solution.py:133
  340.1 34.0 %all_to_all.120 = bf16[16,128,256]{2,1,0:T(8,128)(2,1)S(1)} all-to-all(bf16[16,128,256]{2,1,0:T(8,128)(2,1)} %bitcast.57), channel_id=1, replica_groups=mesh['grp'=16,'sp'=16] {'sp'}, dimensions={0} | all-to-all | bytes 2097152 | tf_op jit(solution)/shard_map/all_to_all | solution.py:135
  374.1 4.4 %all-to-all-start.5 = ((bf16[16,128,256]{2,1,0:T(8,128)(2,1)}), bf16[16,128,256]{2,1,0:T(8,128)(2,1)S(1)}, u32[]{:S(2)}, u32[]{:S(2)}) async-start(bf16[16,128,256]{2,1,0:T(8,128)(2,1)} %bitcast.14), calls=%async_computation.5 | async-start | bytes 2097152 | tf_op jit(solution)/shard_map/all_to_all | solution.py:134
  378.5 1.3 copy.45
  379.8 2.3 copy.48
  382.7 1.3 copy.50
  384.0 21.3 %all-to-all-done.5 = bf16[16,128,256]{2,1,0:T(8,128)(2,1)S(1)} async-done(((bf16[16,128,256]{2,1,0:T(8,128)(2,1)}), bf16[16,128,256]{2,1,0:T(8,128)(2,1)S(1)}, u32[]{:S(2)}, u32[]{:S(2)}) %all-to-all-start.5) | async-done | bytes 1048608 | tf_op jit(solution)/shard_map/all_to_all | solution.py:134
  405.9 1.3 copy.49
  (50 shorter events, 12.0 us)
Async XLA Ops:
  7.2 14.2 %copy-start.1 = (bf16[128,4096]{1,0:T(8,128)(2,1)S(1)}, bf16[128,4096]{1,0:T(8,128)(2,1)}, u32[]{:S(2)}) copy-start(bf16[128,4096]{1,0:T(8,128)(2,1)} %param.16) | copy-start | bytes 3145732
  7.2 232.3 %all-gather.2.cloned.1.call-start = ((), (), s32[]{:S(2)}) async-start(), calls=%async_computation.8 | async-start | bytes 13369344 | tf_op jit(solution)/shard_map/all_gather | solution.py:98
  7.9 62.4 %copy-start.2 = (bf16[128,4096]{1,0:T(8,128)(2,1)S(1)}, bf16[128,4096]{1,0:T(8,128)(2,1)}, u32[]{:S(2)}) copy-start(bf16[128,4096]{1,0:T(8,128)(2,1)} %param.17) | copy-start | bytes 3145732
  10.3 47.4 %all-to-all-start = ((bf16[128,16,256]{2,0,1:T(8,128)(2,1)}), bf16[128,16,256]{2,0,1:T(8,128)(2,1)S(1)}, u32[]{:S(2)}, u32[]{:S(2)}) async-start(bf16[128,16,256]{2,0,1:T(8,128)(2,1)} %bitcast.48), calls=%async_computation | async-start | bytes 2097152 | tf_op jit(solution)/shard_map/all_to_all | solution.py:63
  21.4 83.3 %copy-start.5 = (s32[4]{0:T(128)S(1)}, s32[4]{0:T(128)}, u32[]{:S(2)}) copy-start(s32[4]{0:T(128)} %param.14) | copy-start | bytes 52
  21.4 83.2 %copy-start.6 = (s32[16]{0:T(128)S(1)}, s32[16]{0:T(128)}, u32[]{:S(2)}) copy-start(s32[16]{0:T(128)} %param.12) | copy-start | bytes 196
  21.4 83.2 %copy-start.7 = (s32[4]{0:T(128)S(1)}, s32[4]{0:T(128)}, u32[]{:S(2)}) copy-start(s32[4]{0:T(128)} %param.13) | copy-start | bytes 52
  21.4 132.4 %copy-start.4 = (bf16[256,192]{0,1:T(8,128)(2,1)S(1)}, bf16[256,192]{0,1:T(8,128)(2,1)}, u32[]{:S(2)}) copy-start(bf16[256,192]{0,1:T(8,128)(2,1)} %param.19) | copy-start | bytes 294916
  57.7 40.7 %all-to-all-start.1 = ((bf16[128,16,256]{2,0,1:T(8,128)(2,1)}), bf16[128,16,256]{2,0,1:T(8,128)(2,1)S(1)}, u32[]{:S(2)}, u32[]{:S(2)}) async-start(bf16[128,16,256]{2,0,1:T(8,128)(2,1)} %bitcast.47), calls=%async_computation.1 | async-start | bytes 2097152 | tf_op jit(solution)/shard_map/all_to_all | solution.py:64
  98.4 55.3 %all-to-all-start.3 = ((bf16[128,16,256]{2,0,1:T(8,128)(2,1)}), bf16[128,16,256]{2,0,1:T(8,128)(2,1)S(1)}, u32[]{:S(2)}, u32[]{:S(2)}) async-start(bf16[128,16,256]{2,0,1:T(8,128)(2,1)} %bitcast.46), calls=%async_computation.3 | async-start | bytes 2097152 | tf_op jit(solution)/shard_map/all_to_all | solution.py:65
  153.8 9.4 %copy-start.3 = (bf16[128,16,256]{2,0,1:T(8,128)(2,1)}, bf16[128,16,256]{2,0,1:T(8,128)(2,1)S(1)}, u32[]{:S(2)}) copy-start(bf16[128,16,256]{2,0,1:T(8,128)(2,1)S(1)} %all-to-all-done.3) | copy-start | bytes 3145732
  155.2 95.8 %all-to-all-start.2 = ((bf16[16,256,192]{1,2,0:T(8,128)(2,1)}), bf16[16,256,192]{1,2,0:T(8,128)(2,1)}, u32[]{:S(2)}, u32[]{:S(2)}) async-start(bf16[16,256,192]{1,2,0:T(8,128)(2,1)} %broadcast_in_dim.87), calls=%async_computation.2 | async-start | bytes 3145728 | tf_op jit(solution)/shard_map/all_to_all | solution.py:12
  163.1 244.1 %reduce-scatter.2.cloned.1.call-start = ((), (), s32[]{:S(2)}) async-start(), calls=%async_computation.9 | async-start | bytes 3342336 | tf_op jit(solution)/shard_map/reduce_scatter | solution.py:138
  265.5 1.7 copy-start
  276.1 1.7 copy-start
  286.7 1.7 copy-start
  297.4 1.7 copy-start
  374.1 31.2 %all-to-all-start.5 = ((bf16[16,128,256]{2,1,0:T(8,128)(2,1)}), bf16[16,128,256]{2,1,0:T(8,128)(2,1)S(1)}, u32[]{:S(2)}, u32[]{:S(2)}) async-start(bf16[16,128,256]{2,1,0:T(8,128)(2,1)} %bitcast.14), calls=%async_computation.5 | async-start | bytes 2097152 | tf_op jit(solution)/shard_map/all_to_all | solution.py:134
Sparse Core Ops, SparseCore 0:
  10.4 229.0 all-gather.1
  251.2 61.2 reduce-scatter.1
where the time goes:
time: 415 us; the launch traced here: 414 us
  waiting for transfers between devices  186 us (45%)
  blocking collectives  67.9 us (16%)
  matrix products  65.6 us (16%)
  starting transfers between devices  42.1 us (10%)
  other arithmetic  19.5 us (5%)
  local copies, waits for them, and re-layouts  16.8 us (4%)
  between operations  15.6 us (4%)
    all_gather x1, waiting for transfers between devices, shards(): gathered = lax.all_gather(out_grad, 'sp', axis=0, tiled=True)  56.8 us
    all_to_all x1, waiting for transfers between devices, shards(): lax.all_to_all(values, 'sp', split_axis=1, concat_axis=0, tiled=True)  45.1 us
    all_to_all x1, waiting for transfers between devices, shards(): lax.all_to_all(queries, 'sp', split_axis=1, concat_axis=0, tiled=True)  35.2 us
    all_to_all x1, blocking collectives, shards(): lax.all_to_all(grad_v_all, 'sp', split_axis=0, concat_axis=1, tiled=True)  34 us
    all_to_all x1, blocking collectives, shards(): lax.all_to_all(grad_q_all, 'sp', split_axis=0, concat_axis=1, tiled=True)  33.9 us
    all_to_all x1, waiting for transfers between devices, shards(): lax.all_to_all(keys, 'sp', split_axis=1, concat_axis=0, tiled=True)  27 us
    dot_general x9, matrix products, dot_tn(): lax.dot_general(first_op, second_op, (((0,), (0,)), ((), ())), preferred_...  24.8 us
    dot_general x13, matrix products, dot_nt(): lax.dot_general(first_op, second_op, (((1,), (1,)), ((), ())), preferred_...  24.8 us
  transfers between devices with their start and end apart: 7, of which 5 were waited for; matrix products, arithmetic and copies ran while one was open for 25% of the time, Pallas kernels for 0%

commit v1 on v0

--- a/solution.py
+++ b/solution.py
@@ -95,7 +95,8 @@
     )
     masked = attention * keep_rows[:, None].astype(jnp.bfloat16)
     w_rows = gather_directly(w_out, "grp", 1)
-    gathered = lax.all_gather(out_grad, "sp", axis=0, tiled=True)
+    sent = jnp.stack([out_grad] * lax.axis_size("sp"))
+    gathered = jnp.concatenate(lax.all_to_all(sent, "sp", 0, 0), axis=0)
     d_full = dot_nt(gathered, w_rows)
     grad_local = dot_tn(masked, gathered)
     d_attn = (d_full * row_scale).astype(jnp.bfloat16)

time: 415 us -> 619 us (1.49)
  waiting for transfers between devices: 186 us -> 354 us
  blocking collectives: 67.9 us -> 97.3 us
  local copies, waits for them, and re-layouts: 16.8 us -> 24.1 us
    all_to_all x2, waiting for transfers between devices: 66.4 us -> 301 us  [the longest x1 282 us: shards(): gathered = jnp.concatenate(lax.all_to_all(sent, 'sp', 0, 0), axis=0)]
    all_gather x1 -> x0, waiting for transfers between devices: 56.8 us -> none  [shards(): gathered = lax.all_gather(out_grad, 'sp', axis=0, tiled=True)]
    all_to_all x1 -> x2, blocking collectives: 34 us -> 62.8 us  [the longest x1 34 us: shards(): lax.all_to_all(values, 'sp', split_axis=1, concat_axis=0, tiled=True)]
    all_to_all x1, waiting for transfers between devices: 35.2 us -> 26.8 us  [shards(): lax.all_to_all(queries, 'sp', split_axis=1, concat_axis=0, tiled=True)]
    another operation x4 -> x5, local copies, waits for them, and re-layouts: 3.19 us -> 10.4 us  [the longest x1 7.2 us: shards(): sent = jnp.stack([out_grad] * lax.axis_size('sp'))]
    all_to_all x1, starting transfers between devices: 12.6 us -> 5.95 us  [shards(): lax.all_to_all(keys, 'sp', split_axis=1, concat_axis=0, tiled=True)]
  transfers between devices with their start and end apart: 7 -> 6, of which waited for: 5 -> 4; matrix products, arithmetic and copies ran while one was open for 25% -> 16% of each run, Pallas kernels for 0% -> 0%
where the time goes in v1:
time: 619 us; the launch traced here: 612 us
  waiting for transfers between devices  354 us (57%)
  blocking collectives  97.3 us (16%)
  matrix products  65.8 us (11%)
  starting transfers between devices  38.3 us (6%)
  local copies, waits for them, and re-layouts  24.1 us (4%)
  other arithmetic  16.4 us (3%)
  between operations  15.5 us (3%)
    all_to_all x1, waiting for transfers between devices, shards(): gathered = jnp.concatenate(lax.all_to_all(sent, 'sp', 0, 0), axis=0)  282 us
    all_to_all x1, blocking collectives, shards(): lax.all_to_all(grad_q_all, 'sp', split_axis=0, concat_axis=1, tiled=True)  34.5 us
    all_to_all x1, blocking collectives, shards(): lax.all_to_all(values, 'sp', split_axis=1, concat_axis=0, tiled=True)  34 us
    all_to_all x1, blocking collectives, shards(): lax.all_to_all(grad_k_all, 'sp', split_axis=0, concat_axis=1, tiled=True)  28.8 us
    all_to_all x1, waiting for transfers between devices, shards(): lax.all_to_all(queries, 'sp', split_axis=1, concat_axis=0, tiled=True)  26.8 us
    all_to_all x1, waiting for transfers between devices, shards(): lax.all_to_all(keys, 'sp', split_axis=1, concat_axis=0, tiled=True)  26.2 us
    dot_general x9, matrix products, dot_tn(): lax.dot_general(first_op, second_op, (((0,), (0,)), ((), ())), preferred_...  24.9 us
    dot_general x13, matrix products, dot_nt(): lax.dot_general(first_op, second_op, (((1,), (1,)), ((), ())), preferred_...  24.8 us
  transfers between devices with their start and end apart: 6, of which 4 were waited for; matrix products, arithmetic and copies ran while one was open for 16% of the time, Pallas kernels for 0%

profile of v1, /device:TPU:8, one launch (start us, length us, event | category | flops | bytes accessed | tf_op | source)
XLA Modules:
  0.0 612.0 jit_solution(17398223046747891048)
XLA Ops:
  7.2 2.4 copy.64
  9.6 11.0 %all-to-all-start = ((bf16[128,16,256]{2,0,1:T(8,128)(2,1)}), bf16[128,16,256]{2,0,1:T(8,128)(2,1)S(1)}, u32[]{:S(2)}, u32[]{:S(2)}) async-start(bf16[128,16,256]{2,0,1:T(8,128)(2,1)} %bitcast.49), calls=%async_computation | async-start | bytes 2097152 | tf_op jit(solution)/shard_map/all_to_all | solution.py:63
  20.6 1.1 copy.63
  21.7 26.8 %all-to-all-done = bf16[128,16,256]{2,0,1:T(8,128)(2,1)S(1)} async-done(((bf16[128,16,256]{2,0,1:T(8,128)(2,1)}), bf16[128,16,256]{2,0,1:T(8,128)(2,1)S(1)}, u32[]{:S(2)}, u32[]{:S(2)}) %all-to-all-start) | async-done | bytes 1048608 | tf_op jit(solution)/shard_map/all_to_all | solution.py:63
  48.5 5.9 all-to-all-start.1
  54.4 1.3 copy.62
  55.8 26.2 %all-to-all-done.1 = bf16[128,16,256]{2,0,1:T(8,128)(2,1)S(1)} async-done(((bf16[128,16,256]{2,0,1:T(8,128)(2,1)}), bf16[128,16,256]{2,0,1:T(8,128)(2,1)S(1)}, u32[]{:S(2)}, u32[]{:S(2)}) %all-to-all-start.1) | async-done | bytes 1048608 | tf_op jit(solution)/shard_map/all_to_all | solution.py:64
  82.0 34.0 %all_to_all.124 = bf16[128,16,256]{2,0,1:T(8,128)(2,1)} all-to-all(bf16[128,16,256]{2,0,1:T(8,128)(2,1)S(1)} %bitcast.58), channel_id=1, replica_groups=mesh['grp'=16,'sp'=16] {'sp'}, dimensions={1} | all-to-all | bytes 2097152 | tf_op jit(solution)/shard_map/all_to_all | solution.py:65
  116.0 7.2 %stack.2 = bf16[16,128,3072]{2,1,0:T(8,128)(2,1)} broadcast(bf16[128,3072]{1,0:T(8,128)(2,1)} %param.18), dimensions={1,2} | broadcast | bytes 13369344 | tf_op jit(solution)/shard_map/stack | solution.py:98
  123.2 5.1 all-to-all-start.2
  132.5 282.2 %all-to-all-done.2 = bf16[16,128,3072]{2,1,0:T(8,128)(2,1)} async-done(((bf16[16,128,3072]{2,1,0:T(8,128)(2,1)}), bf16[16,128,3072]{2,1,0:T(8,128)(2,1)}, u32[]{:S(2)}, u32[]{:S(2)}) %all-to-all-start.2) | async-done | bytes 12582944 | tf_op jit(solution)/shard_map/all_to_all | solution.py:99
  414.7 1.3 broadcast_in_dim.87
  416.0 4.9 all-to-all-start.3
  421.3 19.7 %while.36 = (s32[]{:T(128)}, bf16[2048,256]{1,0:T(8,128)(2,1)S(1)}, bf16[2048,256]{1,0:T(8,128)(2,1)S(1)}, bf16[2048,256]{1,0:T(8,128)(2,1)S(1)}, bf16[2048,256]...) while((s32[]{:T(128)}, bf16[2048,256]{1,0:T(8,128)(2,1)S(1)}, ...), condition=%wide.region_5.6_spmd.clone, body=%wide.region_2.5_spmd.clone.sunk | while | flops 549583872 | bytes 13660504 | solution.py:93
  422.0 0.7 fusion.69
  422.7 0.9 fusion.70
  423.6 2.5 fusion.71
  426.9 0.7 fusion.69
  427.7 0.9 fusion.70
  428.6 2.5 fusion.71
  431.9 0.7 fusion.69
  432.6 0.9 fusion.70
  433.5 2.5 fusion.71
  436.8 0.7 fusion.69
  437.5 0.9 fusion.70
  438.5 2.5 fusion.71
  441.0 11.6 %convolution_multiply_fusion.2 = f32[256,3072]{0,1:T(8,128)} fusion(bf16[2048,3072]{1,0:T(8,128)(2,1)} %bitcast.4, f32[]{:T(128)S(6)} %div.66, bf16[2048,256]{1,0:T(8,128)(2,1)S(1)} %get-tuple-element.655, bf16[2048]{0:T(1024)(128)(2,1)S(1)} %bitcast.67), kind=kOutput, calls=%fused_computation.43 | convolution fusion | flops 3222536192 | bytes 16781316 | tf_op jit(solution)/shard_map/dot_general | solution.py:35
  452.6 9.5 %fusion.39 = bf16[2048,256]{1,0:T(8,128)(2,1)} fusion(bf16[2048,3072]{1,0:T(8,128)(2,1)} %bitcast.4, bf16[256,3072]{0,1:T(8,128)(2,1)} %bitcast.6, f32[2048]{0:T(1024)S(1)} %bitcast.66), kind=kOutput, calls=%fused_computation.45 | convolution fusion | flops 3222274048 | bytes 15212544 | tf_op jit(solution)/shard_map/dot_general | solution.py:29
  462.1 1.0 broadcast.64
  463.1 1.0 broadcast.64.clone
  464.1 1.1 broadcast.64.clone.1
  465.2 39.1 %while.37 = (s32[]{:T(128)}, bf16[2048,256]{1,0:T(8,128)(2,1)}, bf16[2048,256]{1,0:T(8,128)(2,1)}, bf16[2048,256]{1,0:T(8,128)(2,1)}, bf16[2048,256]{1,0:T(8,128...) while((s32[]{:T(128)}, bf16[2048,256]{1,0:T(8,128)(2,1)}, ...), condition=%wide.region_10.11_spmd.clone, body=%wide.region_6.10_spmd.clone.sunk | while | flops 1363277824 | bytes 30461340 | solution.py:130
  465.9 0.7 fusion.80
  466.7 0.9 fusion.81
  467.6 1.9 fusion.84
  469.7 2.4 multiply_convert_fusion.2
  472.1 1.4 fusion.83
  473.5 1.5 fusion.82
  475.7 0.7 fusion.80
  476.4 0.9 fusion.81
  477.4 1.9 fusion.84
  479.5 2.4 multiply_convert_fusion.2
  481.8 1.4 fusion.83
  483.3 1.5 fusion.82
  485.5 0.7 fusion.80
  486.2 0.9 fusion.81
  487.1 1.9 fusion.84
  489.3 2.4 multiply_convert_fusion.2
  491.6 1.4 fusion.83
  493.1 1.5 fusion.82
  495.3 0.7 fusion.80
  496.0 0.9 fusion.81
  496.9 1.9 fusion.84
  499.0 2.4 multiply_convert_fusion.2
  501.4 1.4 fusion.83
  502.8 1.5 fusion.82
  504.3 34.5 %all_to_all.125 = bf16[16,128,256]{2,1,0:T(8,128)(2,1)S(1)} all-to-all(bf16[16,128,256]{2,1,0:T(8,128)(2,1)} %bitcast.12), channel_id=1, replica_groups=mesh['grp'=16,'sp'=16] {'sp'}, dimensions={0} | all-to-all | bytes 2097152 | tf_op jit(solution)/shard_map/all_to_all | solution.py:134
  538.8 28.8 %all_to_all.126 = bf16[16,128,256]{2,1,0:T(8,128)(2,1)S(1)} all-to-all(bf16[16,128,256]{2,1,0:T(8,128)(2,1)} %bitcast.15), channel_id=1, replica_groups=mesh['grp'=16,'sp'=16] {'sp'}, dimensions={0} | all-to-all | bytes 2097152 | tf_op jit(solution)/shard_map/all_to_all | solution.py:135
  567.7 11.1 %all-to-all-start.7 = ((bf16[16,128,256]{2,1,0:T(8,128)(2,1)}), bf16[16,128,256]{2,1,0:T(8,128)(2,1)S(1)}, u32[]{:S(2)}, u32[]{:S(2)}) async-start(bf16[16,128,256]{2,1,0:T(8,128)(2,1)} %bitcast.18), calls=%async_computation.7 | async-start | bytes 2097152 | tf_op jit(solution)/shard_map/all_to_all | solution.py:136
  578.8 1.3 copy.45
  580.1 2.3 copy.48
  583.0 1.3 copy.49
  584.3 18.9 %all-to-all-done.7 = bf16[16,128,256]{2,1,0:T(8,128)(2,1)S(1)} async-done(((bf16[16,128,256]{2,1,0:T(8,128)(2,1)}), bf16[16,128,256]{2,1,0:T(8,128)(2,1)S(1)}, u32[]{:S(2)}, u32[]{:S(2)}) %all-to-all-start.7) | async-done | bytes 1048608 | tf_op jit(solution)/shard_map/all_to_all | solution.py:136
  603.9 1.3 copy.50
  (45 shorter events, 10.8 us)
Async XLA Ops:
  7.2 13.4 %copy-start.1 = (bf16[128,4096]{1,0:T(8,128)(2,1)S(1)}, bf16[128,4096]{1,0:T(8,128)(2,1)}, u32[]{:S(2)}) copy-start(bf16[128,4096]{1,0:T(8,128)(2,1)} %param.16) | copy-start | bytes 3145732
  9.6 38.9 %all-to-all-start = ((bf16[128,16,256]{2,0,1:T(8,128)(2,1)}), bf16[128,16,256]{2,0,1:T(8,128)(2,1)S(1)}, u32[]{:S(2)}, u32[]{:S(2)}) async-start(bf16[128,16,256]{2,0,1:T(8,128)(2,1)} %bitcast.49), calls=%async_computation | async-start | bytes 2097152 | tf_op jit(solution)/shard_map/all_to_all | solution.py:63
  48.5 33.5 %all-to-all-start.1 = ((bf16[128,16,256]{2,0,1:T(8,128)(2,1)}), bf16[128,16,256]{2,0,1:T(8,128)(2,1)S(1)}, u32[]{:S(2)}, u32[]{:S(2)}) async-start(bf16[128,16,256]{2,0,1:T(8,128)(2,1)} %bitcast.48), calls=%async_computation.1 | async-start | bytes 2097152 | tf_op jit(solution)/shard_map/all_to_all | solution.py:64
  123.2 5.1 copy-start.3
  123.2 5.1 copy-start.4
  123.2 5.1 copy-start.5
  123.2 291.5 %copy-start.2 = (bf16[256,192]{0,1:T(8,128)(2,1)S(1)}, bf16[256,192]{0,1:T(8,128)(2,1)}, u32[]{:S(2)}) copy-start(bf16[256,192]{0,1:T(8,128)(2,1)} %param.19) | copy-start | bytes 294916
  123.2 291.5 %all-to-all-start.2 = ((bf16[16,128,3072]{2,1,0:T(8,128)(2,1)}), bf16[16,128,3072]{2,1,0:T(8,128)(2,1)}, u32[]{:S(2)}, u32[]{:S(2)}) async-start(bf16[16,128,3072]{2,1,0:T(8,128)(2,1)} %stack.2), calls=%async_computation.2 | async-start | bytes 25165824 | tf_op jit(solution)/shard_map/all_to_all | solution.py:99
  416.0 36.6 %all-to-all-start.3 = ((bf16[16,256,192]{1,2,0:T(8,128)(2,1)}), bf16[16,256,192]{1,2,0:T(8,128)(2,1)}, u32[]{:S(2)}, u32[]{:S(2)}) async-start(bf16[16,256,192]{1,2,0:T(8,128)(2,1)} %broadcast_in_dim.87), calls=%async_computation.3 | async-start | bytes 3145728 | tf_op jit(solution)/shard_map/all_to_all | solution.py:12
  421.0 184.2 %reduce-scatter.2.cloned.1.call-start = ((), (), s32[]{:S(2)}) async-start(), calls=%async_computation.9 | async-start | bytes 3342336 | tf_op jit(solution)/shard_map/reduce_scatter | solution.py:139
  465.9 1.7 copy-start
  475.7 1.7 copy-start
  485.5 1.7 copy-start
  495.2 1.7 copy-start
  567.7 35.5 %all-to-all-start.7 = ((bf16[16,128,256]{2,1,0:T(8,128)(2,1)}), bf16[16,128,256]{2,1,0:T(8,128)(2,1)S(1)}, u32[]{:S(2)}, u32[]{:S(2)}) async-start(bf16[16,128,256]{2,1,0:T(8,128)(2,1)} %bitcast.18), calls=%async_computation.7 | async-start | bytes 2097152 | tf_op jit(solution)/shard_map/all_to_all | solution.py:136
Sparse Core Ops, SparseCore 0:
  452.7 64.4 reduce-scatter.1
